TPU v7x, 32 devices: a whole 2x2x4 slice. The times are simulated.
32 devices in a mesh: pw: 8 (over z, core), band: 4 (over y, x).
Axes of the slice: x: 2, y: 2, z: 4, core: 2. Of those that a mesh axis runs over, the one named last changes fastest.
Arguments:
- wavefunctions: bfloat16 [2, 4096, 512], P(None, 'pw', 'band'), may hold values from -0.09375 to 0.09375
- miller: int32 [3, 4096], P(None, 'pw'), may hold values from -16 to 16
- reciprocal: float32 [3, 3], replicated, may hold values from -0.15 to 1.15, as said below
- fractional: float32 [3, 32], replicated, may hold values from 0 to 1
- species: int32 [32], replicated, may hold values from 0 to 3
- atom_order: int32 [32], replicated, may hold values from 0 to 31, each once
- radial_widths: float32 [4, 4], replicated, may hold values from 0.003 to 0.02
- onsite_base: float32 [4, 8, 8], replicated, may hold values from -2 to 2
- coupling: float32 [4, 64, 64], replicated, may hold values from -0.75 to 0.75
- occupations: float32 [512], P('band'), may hold values from 0 to 3, as said below
Outputs:
- applied: bfloat16 [2, 4096, 512], P(None, 'pw', 'band')
- onsite_d: float32 [32, 8, 8], P('pw')
Inputs may be any that keep to these rules, and one draw needn't show every extreme that they name: `atom_order`: a permutation of the atoms. `reciprocal`: each diagonal entry is 0.85 or more and each other entry 0.15 or less in magnitude. `occupations`: positive.
All inputs are finite; a program needn't handle non-finite values.
Results may differ from a plain program's by a relative error of at most 0.008.
Values may be sent and summed in bfloat16 or wider, within the bound.
A program may use at most 64 MiB of HBM per device.

v0:
```python
import math
import jax
import jax.numpy as jnp
from jax import lax
from jax.sharding import PartitionSpec as P

HIGH = lax.Precision.HIGHEST


def projector_tile(miller_cols, reciprocal, positions, atom_species, radial_widths):
    two_pi = 2.0 * math.pi
    miller_real = miller_cols.astype(jnp.float32)
    g_vectors = two_pi * jnp.dot(reciprocal, miller_real, precision=HIGH)
    g_square = jnp.sum(g_vectors * g_vectors, axis=0)
    phases = two_pi * jnp.dot(positions.T, miller_real, precision=HIGH)
    onehot = (
        atom_species[:, None] == jnp.arange(radial_widths.shape[0], dtype=jnp.int32)[None, :]
    ).astype(jnp.float32)
    widths = jnp.dot(onehot, radial_widths, precision=HIGH)
    radial = jnp.exp(-0.5 * g_square[None, None, :] * (widths * widths)[:, :, None])
    s_part = radial[:, 0:2, :]
    p_first = g_vectors[None, :, :] * (widths[:, 2, None, None] * radial[:, 2:3, :])
    p_second = g_vectors[None, :, :] * (widths[:, 3, None, None] * radial[:, 3:4, :])
    p_part = jnp.concatenate([p_first, p_second], axis=1)
    cosine = jnp.cos(phases)[:, None, :]
    sine = jnp.sin(phases)[:, None, :]
    beta_real = jnp.concatenate([s_part * cosine, -p_part * sine], axis=1)
    beta_imag = jnp.concatenate([-s_part * sine, -p_part * cosine], axis=1)
    rows = positions.shape[1] * 8
    return (
        beta_real.reshape(rows, -1).astype(jnp.bfloat16),
        beta_imag.reshape(rows, -1).astype(jnp.bfloat16),
    )


def project(beta_real, beta_imag, wave_real, wave_imag):
    proj_real = jnp.dot(beta_real, wave_real, preferred_element_type=jnp.float32) + jnp.dot(
        beta_imag, wave_imag, preferred_element_type=jnp.float32
    )
    proj_imag = jnp.dot(beta_real, wave_imag, preferred_element_type=jnp.float32) - jnp.dot(
        beta_imag, wave_real, preferred_element_type=jnp.float32
    )
    return jnp.stack([proj_real, proj_imag], axis=1)


def occupancy_terms(projections, weights):
    grouped = projections.reshape(projections.shape[0] // 8, 8, 2, projections.shape[2])
    return jnp.einsum("aicn,ajcn,n->aij", grouped, grouped, weights, precision=HIGH)


def onsite_matrix(occupancy, atom_species, onsite_base, coupling):
    holding = occupancy.shape[0]
    kinds = onsite_base.shape[0]
    onehot = (atom_species[:, None] == jnp.arange(kinds, dtype=jnp.int32)[None, :]).astype(
        jnp.float32
    )
    response = jnp.einsum("skl,al->ask", coupling, occupancy.reshape(holding, 64), precision=HIGH)
    base = jnp.einsum("as,sk->ak", onehot, onsite_base.reshape(kinds, 64), precision=HIGH)
    total = base + jnp.einsum("as,ask->ak", onehot, response, precision=HIGH)
    return total.reshape(holding, 8, 8)


def weigh(onsite, projections):
    grouped = projections.reshape(projections.shape[0] // 8, 8, 2, projections.shape[2])
    weighted = jnp.einsum("aij,ajcn->aicn", onsite, grouped, precision=HIGH)
    return weighted.reshape(projections.shape).astype(jnp.bfloat16)


def back_project(beta_real, beta_imag, weighted):
    dims = (((0,), (0,)), ((), ()))
    q_real = weighted[:, 0, :]
    q_imag = weighted[:, 1, :]
    out_real = lax.dot_general(
        beta_real, q_real, dims, preferred_element_type=jnp.float32
    ) - lax.dot_general(beta_imag, q_imag, dims, preferred_element_type=jnp.float32)
    out_imag = lax.dot_general(
        beta_real, q_imag, dims, preferred_element_type=jnp.float32
    ) + lax.dot_general(beta_imag, q_real, dims, preferred_element_type=jnp.float32)
    return jnp.stack([out_real, out_imag], axis=0)


def local(
    wavefunctions,
    miller,
    reciprocal,
    fractional,
    species,
    atom_order,
    radial_widths,
    onsite_base,
    coupling,
    occupations,
):
    sorted_species = species[atom_order]
    sorted_positions = fractional[:, atom_order]
    owned_atoms = atom_order.shape[0] // lax.axis_size("pw")
    owner_index = lax.axis_index("pw")
    weights = occupations / (occupations.shape[0] * lax.axis_size("band"))
    wave_real = wavefunctions[0]
    wave_imag = wavefunctions[1]
    positions = sorted_positions
    kinds = sorted_species
    beta_real, beta_imag = projector_tile(miller, reciprocal, positions, kinds, radial_widths)
    projections = lax.psum_scatter(
        project(beta_real, beta_imag, wave_real, wave_imag), "pw", scatter_dimension=0, tiled=True
    )
    own_species = lax.dynamic_slice_in_dim(
        sorted_species, owner_index * owned_atoms, owned_atoms, 0
    )
    occupancy = lax.psum(occupancy_terms(projections, weights), "band")
    onsite_own = onsite_matrix(occupancy, own_species, onsite_base, coupling)
    weighted = weigh(onsite_own, projections)
    positions = sorted_positions
    kinds = sorted_species
    beta_real, beta_imag = projector_tile(miller, reciprocal, positions, kinds, radial_widths)
    applied = back_project(beta_real, beta_imag, lax.all_gather(weighted, "pw", axis=0, tiled=True))
    return (applied.astype(jnp.bfloat16), onsite_own)


def solution(mesh):
    placed = (P(None, "pw", "band"), P(None, "pw"), P(), P(), P(), P(), P(), P(), P(), P("band"))
    return jax.shard_map(
        local,
        mesh=mesh,
        in_specs=placed,
        out_specs=(P(None, "pw", "band"), P("pw", None, None)),
        check_vma=False,
    )
```

profile of v0, /device:TPU:0, one launch (start us, length us, event | category | flops | bytes accessed | tf_op | source)
XLA Modules:
  0.0 84.7 jit_solution(17103418098538546727)
XLA Ops:
  7.2 0.0 copy-start
  7.2 0.0 reduce-scatter.2.cloned.1.call-start
  7.2 0.7 compare_select_fusion
  7.9 0.0 copy-start.1
  7.9 0.6 copy-done.1
  8.6 0.0 copy-start.8
  8.6 0.7 gather_fusion
  9.3 0.0 copy-done.8
  9.3 0.0 copy-start.4
  9.3 0.2 fusion.36
  9.5 0.0 copy-start.6
  9.5 0.5 copy-done.4
  10.0 0.2 copy-done.6
  10.2 0.2 multiply_reduce_fusion
  10.4 0.0 copy-start.7
  10.4 0.1 copy.17
  10.5 0.6 copy-done.7
  11.0 0.1 copy.18
  11.1 0.6 gather_fusion.1
  11.7 0.4 fusion.35
  12.1 0.1 multiply_exponential_fusion
  12.3 0.2 slice_multiply_fusion.1
  12.5 0.1 multiply_convert_fusion.2
  12.6 0.1 broadcast_multiply_fusion.1
  12.7 0.0 copy-start.3
  12.7 0.2 multiply_convert_fusion
  12.9 0.8 copy-done.3
  13.7 0.3 fusion.6
  13.9 0.3 fusion.10
  14.2 0.3 fusion.4
  14.5 0.3 fusion.5
  14.7 0.7 pad_maximum_fusion
  15.5 0.0 copy-start.5
  15.5 0.0 reduce-scatter.2.cloned.1.call-update
  15.5 0.7 copy-done.5
  16.2 0.1 reshape.77
  16.3 0.0 copy-start.9
  16.3 0.1 dynamic_slice.3
  16.3 0.6 copy-done.9
  16.9 0.1 fusion.33
  17.0 32.1 %reduce-scatter.2.cloned.1.call-done = f32[32,2,128]{2,0,1:T(8,128)} async-done(((f32[256,2,128]{2,0,1:T(8,128)}), f32[32,2,128]{2,0,1:T(8,128)}) %reduce-scatter.2.cloned.1.call-update) | async-done | bytes 32784 | tf_op jit(solution)/shard_map/reduce_scatter | solution.py:104
  49.1 1.0 %convolution_bitcast_fusion = f32[4,8,8]{2,1,0:T(8,128)S(1)} fusion(f32[128]{0:T(128)S(1)} %broadcast_multiply_fusion.3, f32[32,2,128]{2,0,1:T(8,128)} %reduce-scatter.2.cloned.1.call-done), kind=kOutput, calls=%fused_computation.14 | convolution fusion | flops 794624 | bytes 34304 | tf_op jit(solution)/shard_map/aicn,ajcn,n->aij/dot_general | solution.py:48
  50.1 0.1 reshape.79
  50.2 9.9 %psum.7 = f32[4,64]{1,0:T(4,128)S(1)} all-reduce(f32[4,64]{1,0:T(4,128)S(1)} %reshape.79), channel_id=1, replica_groups=mesh['pw'=8,'band'=4] {'band'}, use_global_device_ids=true, to_apply=%region_2.0 | all-reduce | flops 256 | bytes 2048 | tf_op jit(solution)/shard_map/psum | solution.py:110
  60.1 0.0 copy-done
  60.1 0.4 fusion.31
  60.5 0.2 fusion.28
  60.6 0.2 convolution_add_fusion.2
  60.8 0.0 copy-start.2
  60.8 0.1 reshape.103
  60.9 0.7 reshape.80
  61.6 0.0 copy-done.2
  61.6 0.2 convolution_convert_fusion
  61.8 14.0 %all_gather.3 = bf16[256,2,128]{2,0,1:T(8,128)(2,1)S(1)} all-gather(bf16[32,2,128]{2,0,1:T(8,128)(2,1)S(1)} %bitcast.79), channel_id=1, replica_groups=mesh['pw'=8,'band'=4] {'pw'}, dimensions={0}, use_global_device_ids=true | all-gather | bytes 147456 | tf_op jit(solution)/shard_map/all_gather | solution.py:116
  75.8 0.3 fusion.17
  76.1 0.3 fusion.16
  76.4 0.3 fusion.2
  76.8 0.3 fusion.3
  77.1 0.7 pad_maximum_fusion.1
  (6 shorter events, 0.0 us)
Async XLA Ops:
  7.2 52.9 %copy-start = (f32[4,64,64]{2,1,0:T(8,128)S(1)}, f32[4,64,64]{2,1,0:T(8,128)}, u32[]{:S(2)}) copy-start(f32[4,64,64]{2,1,0:T(8,128)} %param.18) | copy-start | bytes 196612
  7.2 42.0 %reduce-scatter.2.cloned.1.call-start = ((), (), s32[]{:S(2)}) async-start(), calls=%async_computation.1 | async-start | bytes 294912 | tf_op jit(solution)/shard_map/reduce_scatter | solution.py:104
  7.9 0.7 copy-start.1
  8.6 0.7 copy-start.8
  9.3 0.7 copy-start.4
  9.5 0.7 copy-start.6
  10.4 0.7 copy-start.7
  12.7 1.0 %copy-start.3 = (bf16[2,512,128]{2,1,0:T(8,128)(2,1)S(1)}, bf16[2,512,128]{2,1,0:T(8,128)(2,1)}, u32[]{:S(2)}) copy-start(bf16[2,512,128]{2,1,0:T(8,128)(2,1)} %param.10) | copy-start | bytes 786436
  15.5 0.7 copy-start.5
  16.3 0.7 copy-start.9
  60.8 0.8 copy-start.2
Sparse Core Ops, SparseCore 0:
  15.6 33.4 reduce-scatter.1
where the time goes:
time: 85.2 us; the launch traced here: 84.7 us
  waiting for transfers between devices  32.2 us (38%)
  blocking collectives  23.8 us (28%)
  between operations  14.2 us (17%)
  local copies, waits for them, and re-layouts  6.47 us (8%)
  matrix products  5.02 us (6%)
  other arithmetic  2.96 us (3%)
    reduce_scatter x1, waiting for transfers between devices, local(): lax.psum_scatter(project(beta_real, beta_imag, wave_real, wave_imag), 'pw...  32.1 us
    all_gather x1, blocking collectives, local(): lax.all_gather(weighted, 'pw', axis=0, tiled=True)  14 us
    psum x1, blocking collectives, local(): occupancy = lax.psum(occupancy_terms(projections, weights), 'band')  9.88 us
    unnamed x22, local copies, waits for them, and re-layouts  4.07 us
  transfers between devices with their start and end apart: 1, of which 1 were waited for; matrix products, arithmetic and copies ran while one was open for 0% of the time, Pallas kernels for 0%

commit v1 on v0

--- a/solution.py
+++ b/solution.py
@@ -5,6 +5,13 @@
 from jax.sharding import PartitionSpec as P
 
 HIGH = lax.Precision.HIGHEST
+
+
+def gather_over(block, mesh_axis, along):
+    n_dev = lax.axis_size(mesh_axis)
+    pieces = jnp.stack([block for _ in range(n_dev)])
+    pieces = lax.all_to_all(pieces, mesh_axis, split_axis=0, concat_axis=0)
+    return jnp.concatenate(pieces, axis=along)
 
 
 def projector_tile(miller_cols, reciprocal, positions, atom_species, radial_widths):
@@ -113,7 +120,7 @@
     positions = sorted_positions
     kinds = sorted_species
     beta_real, beta_imag = projector_tile(miller, reciprocal, positions, kinds, radial_widths)
-    applied = back_project(beta_real, beta_imag, lax.all_gather(weighted, "pw", axis=0, tiled=True))
+    applied = back_project(beta_real, beta_imag, gather_over(weighted, "pw", 0))
     return (applied.astype(jnp.bfloat16), onsite_own)
 
 

time: 85.2 us -> 81.9 us (0.961)
  blocking collectives: 23.8 us -> 9.88 us
  waiting for transfers between devices: 32.2 us -> 38.2 us
  starting transfers between devices: 0.04 us -> 3.41 us
  local copies, waits for them, and re-layouts: 6.47 us -> 7.63 us
    all_gather x1 -> x0, blocking collectives: 14 us -> none  [local(): lax.all_gather(weighted, 'pw', axis=0, tiled=True)]
    all_to_all x0 -> x1, waiting for transfers between devices: none -> 6 us  [gather_over(): pieces = lax.all_to_all(pieces, mesh_axis, split_axis=0, concat_axis=0)]
    all_to_all x0 -> x1, starting transfers between devices: none -> 3.37 us  [gather_over(): pieces = lax.all_to_all(pieces, mesh_axis, split_axis=0, concat_axis=0)]
  transfers between devices with their start and end apart: 1 -> 2, of which waited for: 1 -> 2; matrix products, arithmetic and copies ran while one was open for 0% -> 1% of each run, Pallas kernels for 0% -> 0%
where the time goes in v1:
time: 81.9 us; the launch traced here: 81.3 us
  waiting for transfers between devices  38.2 us (47%)
  between operations  14.2 us (17%)
  blocking collectives  9.88 us (12%)
  local copies, waits for them, and re-layouts  7.63 us (9%)
  matrix products  5.03 us (6%)
  starting transfers between devices  3.41 us (4%)
  other arithmetic  2.95 us (4%)
    reduce_scatter x1, waiting for transfers between devices, local(): lax.psum_scatter(project(beta_real, beta_imag, wave_real, wave_imag), 'pw...  32.1 us
    psum x1, blocking collectives, local(): occupancy = lax.psum(occupancy_terms(projections, weights), 'band')  9.88 us
    all_to_all x1, waiting for transfers between devices, gather_over(): pieces = lax.all_to_all(pieces, mesh_axis, split_axis=0, concat_axis=0)  6 us
    unnamed x22, local copies, waits for them, and re-layouts  4.56 us
    all_to_all x1, starting transfers between devices, gather_over(): pieces = lax.all_to_all(pieces, mesh_axis, split_axis=0, concat_axis=0)  3.37 us
  transfers between devices with their start and end apart: 2, of which 2 were waited for; matrix products, arithmetic and copies ran while one was open for 1% of the time, Pallas kernels for 0%

profile of v1, /device:TPU:0, one launch (start us, length us, event | category | flops | bytes accessed | tf_op | source)
XLA Modules:
  0.0 81.3 jit_solution(5538594120152261430)
XLA Ops:
  7.2 0.0 copy-start
  7.2 0.0 reduce-scatter.2.cloned.1.call-start
  7.2 0.7 compare_select_fusion
  7.9 0.0 copy-start.1
  7.9 0.6 copy-done.1
  8.6 0.0 copy-start.8
  8.6 0.7 gather_fusion
  9.3 0.0 copy-done.8
  9.3 0.0 copy-start.4
  9.3 0.2 fusion.36
  9.5 0.0 copy-start.6
  9.5 0.5 copy-done.4
  10.0 0.2 copy-done.6
  10.2 0.2 multiply_reduce_fusion
  10.4 0.0 copy-start.7
  10.4 0.1 copy.23
  10.5 0.6 copy-done.7
  11.0 0.1 copy.24
  11.1 0.6 gather_fusion.1
  11.7 0.4 fusion.35
  12.1 0.1 multiply_exponential_fusion
  12.3 0.2 slice_multiply_fusion.1
  12.5 0.1 multiply_convert_fusion.2
  12.6 0.1 broadcast_multiply_fusion.1
  12.7 0.0 copy-start.3
  12.7 0.2 multiply_convert_fusion
  12.9 0.8 copy-done.3
  13.7 0.3 fusion.6
  13.9 0.3 fusion.10
  14.2 0.3 fusion.4
  14.5 0.3 fusion.5
  14.7 0.7 pad_maximum_fusion
  15.5 0.0 copy-start.5
  15.5 0.0 reduce-scatter.2.cloned.1.call-update
  15.5 0.7 copy-done.5
  16.2 0.1 reshape.83
  16.3 0.0 copy-start.9
  16.3 0.1 dynamic_slice.3
  16.3 0.6 copy-done.9
  16.9 0.1 fusion.33
  17.0 32.1 %reduce-scatter.2.cloned.1.call-done = f32[32,2,128]{2,0,1:T(8,128)} async-done(((f32[256,2,128]{2,0,1:T(8,128)}), f32[32,2,128]{2,0,1:T(8,128)}) %reduce-scatter.2.cloned.1.call-update) | async-done | bytes 32784 | tf_op jit(solution)/shard_map/reduce_scatter | solution.py:111
  49.1 1.0 %convolution_bitcast_fusion = f32[4,8,8]{2,1,0:T(8,128)S(1)} fusion(f32[128]{0:T(128)S(1)} %broadcast_multiply_fusion.3, f32[32,2,128]{2,0,1:T(8,128)} %reduce-scatter.2.cloned.1.call-done), kind=kOutput, calls=%fused_computation.14 | convolution fusion | flops 794624 | bytes 34304 | tf_op jit(solution)/shard_map/aicn,ajcn,n->aij/dot_general | solution.py:55
  50.1 0.1 reshape.85
  50.2 9.9 %psum.7 = f32[4,64]{1,0:T(4,128)S(1)} all-reduce(f32[4,64]{1,0:T(4,128)S(1)} %reshape.85), channel_id=1, replica_groups=mesh['pw'=8,'band'=4] {'band'}, use_global_device_ids=true, to_apply=%region_2.0 | all-reduce | flops 256 | bytes 2048 | tf_op jit(solution)/shard_map/psum | solution.py:117
  60.1 0.0 copy-done
  60.1 0.4 fusion.31
  60.5 0.2 fusion.28
  60.6 0.0 copy-start.2
  60.6 0.2 convolution_add_fusion.2
  60.8 0.1 reshape.110
  60.9 0.5 copy-done.2
  61.4 0.2 convolution_convert_fusion
  61.6 0.7 stack.35
  62.3 3.4 %all-to-all-start = ((bf16[8,32,2,128]{3,1,2,0:T(8,128)(2,1)}), bf16[8,32,2,128]{3,1,2,0:T(8,128)(2,1)S(1)}, u32[]{:S(2)}, u32[]{:S(2)}) async-start(bf16[8,32,2,128]{3,1,2,0:T(8,128)(2,1)} %stack.35), calls=%async_computation.1 | async-start | bytes 262144 | tf_op jit(solution)/shard_map/all_to_all | solution.py:13
  65.6 0.7 reshape.86
  66.3 6.0 %all-to-all-done = bf16[8,32,2,128]{3,1,2,0:T(8,128)(2,1)S(1)} async-done(((bf16[8,32,2,128]{3,1,2,0:T(8,128)(2,1)}), bf16[8,32,2,128]{3,1,2,0:T(8,128)(2,1)S(1)}, u32[]{:S(2)}, u32[]{:S(2)}) %all-to-all-start) | async-done | bytes 131104 | tf_op jit(solution)/shard_map/all_to_all | solution.py:13
  72.3 0.3 fusion.17
  72.7 0.3 fusion.16
  73.0 0.3 fusion.2
  73.4 0.3 fusion.3
  73.7 0.7 pad_maximum_fusion.1
  (7 shorter events, 0.1 us)
Async XLA Ops:
  7.2 52.9 %copy-start = (f32[4,64,64]{2,1,0:T(8,128)S(1)}, f32[4,64,64]{2,1,0:T(8,128)}, u32[]{:S(2)}) copy-start(f32[4,64,64]{2,1,0:T(8,128)} %param.18) | copy-start | bytes 196612
  7.2 41.9 %reduce-scatter.2.cloned.1.call-start = ((), (), s32[]{:S(2)}) async-start(), calls=%async_computation.2 | async-start | bytes 294912 | tf_op jit(solution)/shard_map/reduce_scatter | solution.py:111
  7.9 0.7 copy-start.1
  8.6 0.7 copy-start.8
  9.3 0.7 copy-start.4
  9.5 0.7 copy-start.6
  10.4 0.7 copy-start.7
  12.7 1.0 %copy-start.3 = (bf16[2,512,128]{2,1,0:T(8,128)(2,1)S(1)}, bf16[2,512,128]{2,1,0:T(8,128)(2,1)}, u32[]{:S(2)}) copy-start(bf16[2,512,128]{2,1,0:T(8,128)(2,1)} %param.10) | copy-start | bytes 786436
  15.5 0.7 copy-start.5
  16.3 0.7 copy-start.9
  60.6 0.8 copy-start.2
  62.3 10.1 %all-to-all-start = ((bf16[8,32,2,128]{3,1,2,0:T(8,128)(2,1)}), bf16[8,32,2,128]{3,1,2,0:T(8,128)(2,1)S(1)}, u32[]{:S(2)}, u32[]{:S(2)}) async-start(bf16[8,32,2,128]{3,1,2,0:T(8,128)(2,1)} %stack.35), calls=%async_computation.1 | async-start | bytes 262144 | tf_op jit(solution)/shard_map/all_to_all | solution.py:13
Sparse Core Ops, SparseCore 0:
  15.6 33.4 reduce-scatter.1
